TPU v7x, 128 devices: a whole 4x4x4 slice. The times are simulated.
128 devices in a mesh: px: 16 (over y, z), py: 8 (over x, core).
Axes of the slice: x: 4, y: 4, z: 4, core: 2. Of those that a mesh axis runs over, the one named last changes fastest.
Arguments:
- field: bfloat16 [1, 32, 256, 256, 256], P(None, None, 'px', 'py'), may hold values from -6 to 6
- spectral_weight: bfloat16 [2, 32, 32, 32, 64, 64], P(None, None, 'px', 'py'), may hold values from -72 to 72
- point_weight: bfloat16 [32, 32], replicated, may hold values from -1 to 1
- point_bias: float32 [32], replicated, may hold values from -3 to 3
Outputs:
- layer_out: bfloat16 [1, 32, 256, 256, 256], P(None, None, 'px', 'py')
All inputs are finite; a program needn't handle non-finite values.
Results may differ from a plain program's by a relative error of at most 0.0085.
Values may be sent and summed in bfloat16 or wider, within the bound.
A program may use at most 192 MiB of HBM per device.

v0:
```python
import functools

import jax
import jax.numpy as jnp
import ml_dtypes
import numpy as np
from jax import lax
from jax.experimental import pallas as pl
from jax.experimental.pallas import tpu as pltpu
from jax.sharding import PartitionSpec as P

F32 = jnp.float32
BF16 = jnp.bfloat16
MESH = pl.DeviceIdType.MESH
VMEM_LIMIT = 60 * 1024 * 1024


def split_bf16(table):
    high = table.astype(ml_dtypes.bfloat16)
    low = (table - high.astype(np.float64)).astype(ml_dtypes.bfloat16)
    return high, low


def waves(numbers, positions):
    turns = (np.outer(numbers, positions) % 256).astype(np.float64)
    angle = 2.0 * np.pi * turns / 256.0
    return np.cos(angle), np.sin(angle)


def build_tables():
    signed = np.concatenate([np.arange(32), np.arange(32) - 32])
    grid = np.arange(256)
    cos_z, sin_z = waves(np.arange(32), grid)
    z_rows = np.stack([cos_z.reshape(8, 4, 256), -sin_z.reshape(8, 4, 256)], axis=1).reshape(64, 256)
    z_table = np.concatenate(split_bf16(z_rows), axis=0)
    cos_y, sin_y = waves(signed, grid)
    both = np.stack([cos_y, sin_y], axis=0).transpose(2, 0, 1).reshape(8, 32, 2, 64)
    y_table = np.zeros((8, 4, 32, 2, 4, 64))
    for x in range(4):
        y_table[:, x, :, :, x, :] = both
    y_table = y_table.reshape(1024, 512).astype(ml_dtypes.bfloat16)
    r16 = np.arange(16)
    x_of = (16 * np.arange(16)[:, None] + (2 * (r16 % 8) + r16 // 8)[None, :]).reshape(256)
    cos_x, sin_x = waves(signed, x_of)
    x_table = np.concatenate(split_bf16(np.concatenate([cos_x, sin_x], axis=0)), axis=0)
    cos_x, sin_x = waves(signed, grid)
    xi_table = np.concatenate(split_bf16(np.concatenate([cos_x.T, sin_x.T], axis=0)), axis=1)
    c = cos_y.reshape(64, 8, 32)
    s = sin_y.reshape(64, 8, 32)
    yi_table = np.zeros((4, 2, 64, 2, 8, 4, 32))
    for x in range(4):
        yi_table[x, 0, :, 0, :, x, :] = c
        yi_table[x, 1, :, 0, :, x, :] = -s
        yi_table[x, 0, :, 1, :, x, :] = s
        yi_table[x, 1, :, 1, :, x, :] = c
    yi_table = yi_table.reshape(512, 2048).astype(ml_dtypes.bfloat16)
    factor = np.where(np.arange(32) == 0, 1.0, 2.0)[:, None] / 16777216.0
    back = np.stack([(factor * cos_z).reshape(8, 4, 256), (-factor * sin_z).reshape(8, 4, 256)], axis=1)
    zi = np.zeros((8, 2, 2, 4, 2, 256))
    for o in range(2):
        zi[:, :, o, :, o, :] = back
    zi_table = np.concatenate(split_bf16(zi.reshape(128, 512)), axis=0)
    return z_table, y_table, x_table, xi_table, yi_table, zi_table


def dot(a, b):
    return jnp.dot(a, b, preferred_element_type=F32)


def z_forward(field_ref, table_ref, out_ref):
    for c in range(field_ref.shape[0]):
        rows = field_ref[c].reshape(512, 256)
        both = lax.dot_general(
            table_ref[...], rows, (((1,), (1,)), ((), ())), preferred_element_type=F32
        )
        out_ref[:, c] = (both[:64] + both[64:]).reshape(8, 8, 512).astype(BF16)


def y_forward(in_ref, table_ref, out_ref, rows_ref):
    cb = in_ref.shape[1]
    lower = lax.broadcasted_iota(jnp.int32, (cb, 8, 256), 1) < 4
    for quad in range(4):
        left = jnp.concatenate(
            [in_ref[p, :, :, quad * 128 : (quad + 1) * 128].reshape(cb * 8, 128) for p in range(8)],
            axis=1,
        )
        both = dot(left, table_ref[...])
        turned = pltpu.roll(both[:, 256:].reshape(cb, 8, 256), 4, 1)
        value = both[:, :256].reshape(cb, 8, 256) + jnp.where(lower, turned, -turned)
        value = value.reshape(cb * 8, 256)
        rows_ref[pl.ds(2 * quad, cb * 8, stride=8), :] = value[:, :128]
        rows_ref[pl.ds(2 * quad + 1, cb * 8, stride=8), :] = value[:, 128:]
    rows = rows_ref[...].reshape(cb, 2, 4, 8, 128)
    real = rows[:, 0].reshape(cb * 32, 128)
    imag = rows[:, 1].reshape(cb * 32, 128)
    first = lax.broadcasted_iota(jnp.int32, (cb * 32, 128), 1) < 64
    even = jnp.where(first, real, pltpu.roll(imag, 64, 1)).reshape(cb, 4, 8, 128)
    odd = jnp.where(first, pltpu.roll(real, 64, 1), imag).reshape(cb, 4, 8, 128)
    out_ref[...] = jnp.concatenate([even, odd], axis=2).astype(BF16).reshape(out_ref.shape)


def x_forward(in_ref, table_ref, out_ref):
    first = lax.broadcasted_iota(jnp.int32, (64, 128), 1) < 64
    for c in range(2):
        for l in range(4):
            both = dot(table_ref[...], in_ref[:, c, l].reshape(256, 128))
            both = both[:128] + both[128:]
            turned = pltpu.roll(both[64:], 64, 1)
            out_ref[c, l] = (both[:64] + jnp.where(first, turned, -turned)).astype(BF16)


def mix_channels(spec_ref, weight_ref, l):
    def step(c, sums):
        value = spec_ref[c // 2, c % 2, l].astype(F32)
        real = value[:, :64]
        imag = pltpu.roll(value, 64, 1)[:, :64]
        out = []
        for o in range(2):
            wr = weight_ref[0, c, o, l].astype(F32)
            wi = weight_ref[1, c, o, l].astype(F32)
            out.append(sums[2 * o] + (real * wr - imag * wi))
            out.append(sums[2 * o + 1] + (real * wi + imag * wr))
        return tuple(out)

    zero = jnp.zeros((64, 64), F32)
    return lax.fori_loop(0, 32, step, (zero,) * 4)


def x_inverse(spec_ref, weight_ref, table_ref, out_ref, rows_ref):
    first = lax.broadcasted_iota(jnp.int32, (256, 128), 1) < 64
    for l in range(4):
        sums = mix_channels(spec_ref, weight_ref, l)
        for o in range(2):
            mixed = jnp.concatenate([sums[2 * o], sums[2 * o + 1]], axis=1).astype(BF16)
            both = dot(table_ref[...], jnp.concatenate([mixed, mixed], axis=0))
            turned = pltpu.roll(both[256:], 64, 1)
            value = both[:256] + jnp.where(first, -turned, turned)
            rows_ref[pl.ds(o * 4 + l, 256, stride=8), :] = value
    out_ref[...] = rows_ref[...].astype(BF16).reshape(out_ref.shape)


def y_inverse(in_ref, table_ref, out_ref):
    for quad in range(4):
        left = jnp.concatenate(
            [in_ref[:, (quad * 4 + x) * 8 : (quad * 4 + x + 1) * 8, :].reshape(128, 128) for x in range(4)],
            axis=1,
        )
        for ri in range(2):
            value = dot(left, table_ref[:, ri * 1024 : (ri + 1) * 1024]).reshape(16, 8, 1024).astype(BF16)
            for q in range(8):
                out_ref[q, :, ri, :, quad * 128 : (quad + 1) * 128] = value[:, :, q * 128 : (q + 1) * 128]


def finish(field_ref, spec_ref, point_ref, bias_ref, table_ref, out_ref, point_out):
    for x in range(4):
        for y in range(4):
            rows = field_ref[:, x, y * 8 : (y + 1) * 8, :].reshape(256, 256)
            value = dot(point_ref[...], rows) + bias_ref[...]
            point_out[:, x, y * 8 : (y + 1) * 8, :] = value.reshape(32, 8, 256)

    def step(pair, carry):
        g = spec_ref[:, pair].reshape(128, 128)
        value = lax.dot_general(
            jnp.concatenate([g, g], axis=0),
            table_ref[...],
            (((0,), (0,)), ((), ())),
            preferred_element_type=F32,
        )
        for o in range(2):
            total = value[:, o * 256 : (o + 1) * 256].reshape(4, 32, 256) + point_out[2 * pair + o]
            total = 0.5 * total * (1.0 + lax.erf(total * 0.7071067811865476))
            out_ref[2 * pair + o] = total.astype(BF16)
        return carry

    lax.fori_loop(0, 16, step, 0)


def exchange_kernel(axis, size, gather, in_ref, out_ref, send_sem, recv_sem):
    me = lax.axis_index(axis)
    barrier = pltpu.get_barrier_semaphore()
    for d in range(1, size):
        peer = lax.rem(me + d, size)
        pl.semaphore_signal(barrier, inc=1, device_id={axis: peer}, device_id_type=MESH)
    pl.semaphore_wait(barrier, size - 1)

    def copy(d, peer, slot):
        return pltpu.make_async_remote_copy(
            src_ref=in_ref if gather else in_ref.at[peer],
            dst_ref=out_ref.at[slot],
            send_sem=send_sem.at[d],
            recv_sem=recv_sem.at[d],
            device_id={axis: peer},
            device_id_type=MESH,
        )

    for d in range(1, size):
        copy(d, lax.rem(me + d, size), me).start()
    out_ref[me] = in_ref[...] if gather else in_ref[me]
    for d in range(1, size):
        copy(d, lax.rem(me + d, size), lax.rem(me + size - d, size)).wait()


def exchange(value, axis, size, gather, number):
    shape = (size, *value.shape) if gather else value.shape
    return pl.pallas_call(
        functools.partial(exchange_kernel, axis, size, gather),
        out_shape=jax.ShapeDtypeStruct(shape, value.dtype),
        in_specs=[pl.BlockSpec(memory_space=pltpu.VMEM)],
        out_specs=pl.BlockSpec(memory_space=pltpu.VMEM),
        scratch_shapes=[pltpu.SemaphoreType.DMA((size,)), pltpu.SemaphoreType.DMA((size,))],
        compiler_params=pltpu.CompilerParams(
            collective_id=number, has_side_effects=True, vmem_limit_bytes=VMEM_LIMIT
        ),
        name=f"exchange{number}",
    )(value)


def whole(kernel, out_shape, *args, scratch=(), name=None):
    vm = pl.BlockSpec(memory_space=pltpu.VMEM)
    return pl.pallas_call(
        kernel,
        out_shape=jax.ShapeDtypeStruct(out_shape, BF16),
        in_specs=[vm] * len(args),
        out_specs=vm,
        scratch_shapes=list(scratch),
        compiler_params=pltpu.CompilerParams(vmem_limit_bytes=VMEM_LIMIT),
        name=name,
    )(*args)


def body(tables, field, spectral_weight, point_weight, point_bias):
    z_table, y_table, x_table, xi_table, yi_table, zi_table = tables
    field = field.reshape(32, 16, 32, 256)
    along_z = pl.pallas_call(
        z_forward,
        grid=(8,),
        out_shape=jax.ShapeDtypeStruct((8, 32, 8, 512), BF16),
        in_specs=[
            pl.BlockSpec((4, 16, 32, 256), lambda c: (c, 0, 0, 0)),
            pl.BlockSpec((128, 256), lambda c: (0, 0)),
        ],
        out_specs=pl.BlockSpec((8, 4, 8, 512), lambda c: (0, c, 0, 0)),
        compiler_params=pltpu.CompilerParams(vmem_limit_bytes=VMEM_LIMIT),
        name="z_forward",
    )(field, z_table)
    moved = exchange(along_z, "py", 8, False, 1)
    along_y = pl.pallas_call(
        y_forward,
        grid=(4,),
        out_shape=jax.ShapeDtypeStruct((16, 2, 4, 16, 128), BF16),
        in_specs=[
            pl.BlockSpec((8, 8, 8, 512), lambda c: (0, c, 0, 0)),
            pl.BlockSpec((1024, 512), lambda c: (0, 0)),
        ],
        out_specs=pl.BlockSpec((4, 2, 4, 16, 128), lambda c: (c, 0, 0, 0, 0)),
        scratch_shapes=[pltpu.VMEM((512, 128), F32)],
        compiler_params=pltpu.CompilerParams(vmem_limit_bytes=VMEM_LIMIT),
        name="y_forward",
    )(moved, y_table)
    moved = exchange(along_y, "px", 16, False, 2)
    spectrum = whole(x_forward, (2, 4, 64, 128), moved, x_table, name="x_forward")
    gathered = exchange(spectrum, "px", 16, True, 3)
    mixed = whole(
        x_inverse,
        (16, 128, 128),
        gathered,
        spectral_weight,
        xi_table,
        scratch=[pltpu.VMEM((2048, 128), F32)],
        name="x_inverse",
    )
    moved = exchange(mixed, "px", 16, False, 4)
    back = whole(y_inverse, (8, 16, 2, 8, 512), moved, yi_table, name="y_inverse")
    moved = exchange(back, "py", 8, False, 5)
    point = jnp.kron(point_weight.astype(F32), jnp.eye(8, dtype=F32)).astype(BF16)
    bias = jnp.repeat(point_bias, 8)[:, None]
    out = pl.pallas_call(
        finish,
        grid=(4,),
        out_shape=jax.ShapeDtypeStruct((32, 16, 32, 256), BF16),
        in_specs=[
            pl.BlockSpec((32, 4, 32, 256), lambda x: (0, x, 0, 0)),
            pl.BlockSpec((8, 16, 2, 8, 128), lambda x: (0, 0, 0, 0, x)),
            pl.BlockSpec((256, 256), lambda x: (0, 0)),
            pl.BlockSpec((256, 1), lambda x: (0, 0)),
            pl.BlockSpec((256, 512), lambda x: (0, 0)),
        ],
        out_specs=pl.BlockSpec((32, 4, 32, 256), lambda x: (0, x, 0, 0)),
        scratch_shapes=[pltpu.VMEM((32, 4, 32, 256), F32)],
        compiler_params=pltpu.CompilerParams(vmem_limit_bytes=VMEM_LIMIT),
        name="finish",
    )(field, moved, point, bias, zi_table)
    return out.reshape(1, 32, 16, 32, 256)


def solution(mesh):
    tables = tuple(jnp.asarray(t) for t in build_tables())

    def run(field, spectral_weight, point_weight, point_bias):
        return jax.shard_map(
            body,
            mesh=mesh,
            in_specs=((P(),) * 6, P(None, None, "px", "py", None), P(None, None, "px", "py", None, None), P(), P()),
            out_specs=P(None, None, "px", "py", None),
            check_vma=False,
        )(tables, field, spectral_weight, point_weight, point_bias)

    return run
```

profile of v0, /device:TPU:1, one launch (start us, length us, event | category | flops | bytes accessed | tf_op | source)
XLA Modules:
  0.0 207.6 jit_solution(13000420444831688078)
XLA Ops:
  0.0 0.7 convert_element_type.15
  0.7 0.7 broadcast_in_dim.7
  1.4 0.7 broadcast_in_dim_reshape.4.bias_ref
  2.2 0.4 multiply_convert_fusion
  2.6 3.5 %convert_element_type.18.point_ref = bf16[256,256]{1,0:T(8,128)(2,1)} reshape(bf16[32,8,32,8]{3,2,1,0:T(8,128)(2,1)S(1)} %multiply_convert_fusion) | data formatting | bytes 262144 | tf_op jit(solution)/shard_map/convert_element_type | solution.py:275
  6.1 8.7 %z_forward.1.in_ref = bf16[8,32,8,512]{3,2,1,0:T(8,128)(2,1)} custom-call(bf16[32,16,32,256]{3,2,1,0:T(8,128)(2,1)} %bitcast.4, bf16[128,256]{1,0:T(8,128)(2,1)} %constant.12.clone.table_ref), custom_call_target="tpu_custom_call" | custom-call | tf_op jit(solution)/shard_map/z_forward/pallas_call | solution.py:234
  14.7 31.5 %exchange1.1.in_ref = bf16[8,32,8,512]{3,2,1,0:T(8,128)(2,1)} custom-call(bf16[8,32,8,512]{3,2,1,0:T(8,128)(2,1)} %z_forward.1.in_ref), custom_call_target="tpu_custom_call" | custom-call | tf_op jit(solution)/shard_map/exchange1/pallas_call | solution.py:205
  46.3 6.1 %y_forward.1.in_ref = bf16[16,2,4,16,128]{4,3,2,1,0:T(8,128)(2,1)} custom-call(bf16[8,32,8,512]{3,2,1,0:T(8,128)(2,1)} %exchange1.1.in_ref, bf16[1024,512]{1,0:T(8,128)(2,1)} %constant.13.clone.table_ref), custom_call_target="tpu_custom_call" | custom-call | tf_op jit(solution)/shard_map/y_forward/pallas_call | solution.py:247
  52.4 15.0 %exchange2.1.in_ref = bf16[16,2,4,16,128]{4,3,2,1,0:T(8,128)(2,1)} custom-call(bf16[16,2,4,16,128]{4,3,2,1,0:T(8,128)(2,1)} %y_forward.1.in_ref), custom_call_target="tpu_custom_call" | custom-call | tf_op jit(solution)/shard_map/exchange2/pallas_call | solution.py:205
  67.4 2.2 %x_forward.1.in_ref = bf16[2,4,64,128]{3,2,1,0:T(8,128)(2,1)} custom-call(bf16[16,2,4,16,128]{4,3,2,1,0:T(8,128)(2,1)} %exchange2.1.in_ref, bf16[256,256]{1,0:T(8,128)(2,1)} %constant.14.clone.table_ref), custom_call_target="tpu_custom_call" | custom-call | tf_op jit(solution)/shard_map/x_forward/pallas_call | solution.py:220
  69.6 41.5 %exchange3.1.spec_ref = bf16[16,2,4,64,128]{4,3,2,1,0:T(8,128)(2,1)} custom-call(bf16[2,4,64,128]{3,2,1,0:T(8,128)(2,1)} %x_forward.1.in_ref), custom_call_target="tpu_custom_call" | custom-call | tf_op jit(solution)/shard_map/exchange3/pallas_call | solution.py:205
  111.1 19.5 %x_inverse.1.in_ref = bf16[16,128,128]{2,1,0:T(8,128)(2,1)} custom-call(bf16[16,2,4,64,128]{4,3,2,1,0:T(8,128)(2,1)} %exchange3.1.spec_ref, bf16[2,32,2,4,64,64]{5,4,3,2,1,0:T(8,128)(2,1)} %weight_ref.1, bf16[512,128]{1,0:T(8,128)(2,1)} %constant.15.clone.table_ref), custom_call_target="tpu_custom_call" | custom-call | tf_op jit(solution)/shard_map/x_inverse/pallas_call | solution.py:220
  130.6 17.4 %exchange4.1.in_ref = bf16[16,128,128]{2,1,0:T(8,128)(2,1)} custom-call(bf16[16,128,128]{2,1,0:T(8,128)(2,1)} %x_inverse.1.in_ref), custom_call_target="tpu_custom_call" | custom-call | tf_op jit(solution)/shard_map/exchange4/pallas_call | solution.py:205
  148.0 4.5 %y_inverse.1.in_ref = bf16[8,16,2,8,512]{4,3,2,1,0:T(8,128)(2,1)} custom-call(bf16[16,128,128]{2,1,0:T(8,128)(2,1)} %exchange4.1.in_ref, bf16[512,2048]{1,0:T(8,128)(2,1)} %constant.16.clone.table_ref), custom_call_target="tpu_custom_call" | custom-call | tf_op jit(solution)/shard_map/y_inverse/pallas_call | solution.py:220
  152.5 33.4 %exchange5.1.spec_ref = bf16[8,16,2,8,512]{4,3,2,1,0:T(8,128)(2,1)} custom-call(bf16[8,16,2,8,512]{4,3,2,1,0:T(8,128)(2,1)} %y_inverse.1.in_ref), custom_call_target="tpu_custom_call" | custom-call | tf_op jit(solution)/shard_map/exchange5/pallas_call | solution.py:205
  185.9 21.8 %finish.1 = bf16[32,16,32,256]{3,2,1,0:T(8,128)(2,1)} custom-call(bf16[32,16,32,256]{3,2,1,0:T(8,128)(2,1)} %bitcast.5, bf16[8,16,2,8,512]{4,3,2,1,0:T(8,128)(2,1)} %exchange5.1.spec_ref, bf16[256,256]{1,0:T(8,128)(2,1)} %convert_element_type.18.point_ref, f32[256,1]{1,0:T(8,128)} %broadcast_in_dim_reshape.4.bias_ref, bf16[256,512]{1,0:T(8,128)(2,1)} %constant.17.clone.table_ref), custom_call_target="tpu_custom_call" | custom-call | tf_op jit(solution)/shard_map/finish/pallas_call | solution.py:277
  (1 shorter events, 0.0 us)
where the time goes:
time: 208 us
  Pallas kernels  202 us (97%)
  local copies, waits for them, and re-layouts  4.96 us (2%)
    pallas_call x5, Pallas kernels, exchange(): pl.pallas_call(functools.partial(exchange_kernel, axis, size, gather), ou...  139 us
    pallas_call x3, Pallas kernels, whole(): pl.pallas_call(kernel, out_shape=jax.ShapeDtypeStruct(out_shape, BF16), i...  26.2 us
    pallas_call x1, Pallas kernels, body(): pl.pallas_call(finish, grid=(4,), out_shape=jax.ShapeDtypeStruct((32, 16,...  21.8 us
    pallas_call x1, Pallas kernels, body(): pl.pallas_call(z_forward, grid=(8,), out_shape=jax.ShapeDtypeStruct((8, 3...  8.68 us
    pallas_call x1, Pallas kernels, body(): pl.pallas_call(y_forward, grid=(4,), out_shape=jax.ShapeDtypeStruct((16,...  6.06 us

commit v1 on v0

v1 whole, which is shorter than its diff:
```python
import functools

import jax
import jax.numpy as jnp
import ml_dtypes
import numpy as np
from jax import lax
from jax.experimental import pallas as pl
from jax.experimental.pallas import tpu as pltpu
from jax.sharding import PartitionSpec as P

F32 = jnp.float32
BF16 = jnp.bfloat16
MESH = pl.DeviceIdType.MESH
VMEM_LIMIT = 60 * 1024 * 1024


def split_bf16(table):
    high = table.astype(ml_dtypes.bfloat16)
    low = (table - high.astype(np.float64)).astype(ml_dtypes.bfloat16)
    return high, low


def waves(numbers, positions):
    turns = (np.outer(numbers, positions) % 256).astype(np.float64)
    angle = 2.0 * np.pi * turns / 256.0
    return np.cos(angle), np.sin(angle)


def build_tables():
    signed = np.concatenate([np.arange(32), np.arange(32) - 32])
    grid = np.arange(256)
    cos_z, sin_z = waves(np.arange(32), grid)
    z_rows = np.stack([cos_z.reshape(8, 4, 256), -sin_z.reshape(8, 4, 256)], axis=1).reshape(64, 256)
    z_table = np.concatenate(split_bf16(z_rows), axis=0)
    cos_y, sin_y = waves(signed, grid)
    both = np.stack([cos_y, sin_y], axis=0).transpose(2, 0, 1).reshape(8, 32, 2, 64)
    y_table = np.zeros((8, 4, 32, 2, 4, 64))
    for x in range(4):
        y_table[:, x, :, :, x, :] = both
    y_table = y_table.reshape(1024, 512).astype(ml_dtypes.bfloat16)
    r16 = np.arange(16)
    x_of = (16 * np.arange(16)[:, None] + (2 * (r16 % 8) + r16 // 8)[None, :]).reshape(256)
    cos_x, sin_x = waves(signed, x_of)
    x_table = np.concatenate(split_bf16(np.concatenate([cos_x, sin_x], axis=0)), axis=0)
    cos_x, sin_x = waves(signed, grid)
    xi_table = np.concatenate(split_bf16(np.concatenate([cos_x.T, sin_x.T], axis=0)), axis=1)
    c = cos_y.reshape(64, 8, 32)
    s = sin_y.reshape(64, 8, 32)
    yi_table = np.zeros((4, 2, 64, 2, 8, 4, 32))
    for x in range(4):
        yi_table[x, 0, :, 0, :, x, :] = c
        yi_table[x, 1, :, 0, :, x, :] = -s
        yi_table[x, 0, :, 1, :, x, :] = s
        yi_table[x, 1, :, 1, :, x, :] = c
    yi_table = yi_table.reshape(512, 2048).astype(ml_dtypes.bfloat16)
    factor = np.where(np.arange(32) == 0, 1.0, 2.0)[:, None] / 16777216.0
    back = np.stack([(factor * cos_z).reshape(8, 4, 256), (-factor * sin_z).reshape(8, 4, 256)], axis=1)
    zi = np.zeros((8, 2, 2, 4, 2, 256))
    for o in range(2):
        zi[:, :, o, :, o, :] = back
    zi_table = np.concatenate(split_bf16(zi.reshape(128, 512)), axis=0)
    return z_table, y_table, x_table, xi_table, yi_table, zi_table


def dot(a, b):
    return jnp.dot(a, b, preferred_element_type=F32)


def z_group(field_ref, table_ref, out_ref, group):
    for c in range(4):
        rows = field_ref[group * 4 + c].reshape(512, 256)
        both = lax.dot_general(
            table_ref[...], rows, (((1,), (1,)), ((), ())), preferred_element_type=F32
        )
        out_ref[:, group * 4 + c] = (both[:64] + both[64:]).reshape(8, 8, 512).astype(BF16)


def y_group(in_ref, table_ref, out_ref, rows_ref, group):
    part = pl.ds(group * 4, 4)
    left = jnp.concatenate(
        [
            jnp.concatenate(
                [in_ref[p, part, :, quad * 128 : (quad + 1) * 128].reshape(32, 128) for p in range(8)],
                axis=1,
            )
            for quad in range(4)
        ],
        axis=0,
    )
    both = dot(left, table_ref[...])
    turned = pltpu.roll(both[:, 256:].reshape(16, 8, 256), 4, 1)
    lower = lax.broadcasted_iota(jnp.int32, (16, 8, 256), 1) < 4
    value = both[:, :256].reshape(16, 8, 256) + jnp.where(lower, turned, -turned)
    value = value.reshape(128, 256)
    for quad in range(4):
        rows_ref[pl.ds(2 * quad, 32, stride=8), :] = value[quad * 32 : (quad + 1) * 32, :128]
        rows_ref[pl.ds(2 * quad + 1, 32, stride=8), :] = value[quad * 32 : (quad + 1) * 32, 128:]
    rows = rows_ref[...].reshape(4, 2, 4, 8, 128)
    real = rows[:, 0].reshape(128, 128)
    imag = rows[:, 1].reshape(128, 128)
    first = lax.broadcasted_iota(jnp.int32, (128, 128), 1) < 64
    even = jnp.where(first, real, pltpu.roll(imag, 64, 1)).reshape(4, 4, 8, 128)
    odd = jnp.where(first, pltpu.roll(real, 64, 1), imag).reshape(4, 4, 8, 128)
    out_ref[pl.ds(group * 2, 2)] = (
        jnp.concatenate([even, odd], axis=2).astype(BF16).reshape(2, 2, 4, 16, 128)
    )


def x_forward(in_ref, table_ref, out_ref, me):
    first = lax.broadcasted_iota(jnp.int32, (64, 128), 1) < 64
    for c in range(2):
        for l in range(4):
            both = dot(table_ref[...], in_ref[:, c, l].reshape(256, 128))
            both = both[:128] + both[128:]
            turned = pltpu.roll(both[64:], 64, 1)
            out_ref[me, c, l] = (both[:64] + jnp.where(first, turned, -turned)).astype(BF16)


def mix_channel(spec_ref, weight_ref, sum_ref, p, h, fresh=False):
    c = 2 * p + h
    for l in range(4):
        value = spec_ref[p, h, l].astype(F32)
        real = value[:, :64]
        imag = pltpu.roll(value, 64, 1)[:, :64]
        for o in range(2):
            wr = weight_ref[0, c, o, l].astype(F32)
            wi = weight_ref[1, c, o, l].astype(F32)
            mr = real * wr - imag * wi
            mi = real * wi + imag * wr
            if fresh:
                sum_ref[o, l, 0] = mr
                sum_ref[o, l, 1] = mi
            else:
                sum_ref[o, l, 0] += mr
                sum_ref[o, l, 1] += mi


def x_inverse(sum_ref, table_ref, out_ref, rows_ref):
    first = lax.broadcasted_iota(jnp.int32, (256, 128), 1) < 64
    for o in range(2):
        for l in range(4):
            mixed = jnp.concatenate([sum_ref[o, l, 0], sum_ref[o, l, 1]], axis=1).astype(BF16)
            both = dot(table_ref[...], jnp.concatenate([mixed, mixed], axis=0))
            turned = pltpu.roll(both[256:], 64, 1)
            rows_ref[pl.ds(o * 4 + l, 256, stride=8), :] = both[:256] + jnp.where(first, -turned, turned)
    out_ref[...] = rows_ref[...].astype(BF16).reshape(out_ref.shape)


def y_inverse(in_ref, table_ref, out_ref, group):
    part = pl.ds(group * 4, 4)
    left = jnp.concatenate(
        [
            jnp.concatenate(
                [in_ref[part, (quad * 4 + x) * 8 : (quad * 4 + x + 1) * 8, :].reshape(32, 128) for x in range(4)],
                axis=1,
            )
            for quad in range(4)
        ],
        axis=0,
    )
    for ri in range(2):
        value = dot(left, table_ref[:, ri * 1024 : (ri + 1) * 1024]).reshape(4, 4, 8, 1024).astype(BF16)
        for q in range(8):
            for quad in range(4):
                out_ref[q, part, ri, :, quad * 128 : (quad + 1) * 128] = value[quad, :, :, q * 128 : (q + 1) * 128]


def transform(
    field_hbm, weight_hbm, zt_hbm, yt_hbm, xt_hbm, xit_hbm, yit_hbm, out_hbm,
    field, weight, zt, yt, xt, xit, yit,
    z_out, y_in, y_rows, y_out, x_in, spec, sums, m_rows, m_out, b_in, b_out,
    load_sem, field_sem, s1, r1, s2, r2, s3, r3, s4, r4, s5, r5, own_sem,
):
    px = lax.axis_index("px")
    py = lax.axis_index("py")
    row = px // 4
    col = lax.rem(px, 4)

    def wrap(value, size):
        return lax.rem(value + size, size)

    first_group = wrap(px // 2 + 1, 8)

    def channel_group(step):
        return wrap(first_group + step, 8)

    def load_field(step):
        part = pl.ds(channel_group(step) * 4, 4)
        return pltpu.make_async_copy(field_hbm.at[part], field.at[part], field_sem.at[step])

    loads = [
        pltpu.make_async_copy(a, b, load_sem.at[n])
        for n, (a, b) in enumerate(
            ((zt_hbm, zt), (yt_hbm, yt), (xt_hbm, xt), (weight_hbm, weight), (xit_hbm, xit), (yit_hbm, yit))
        )
    ]
    loads[0].start()
    for step in range(8):
        load_field(step).start()
    for load in loads[1:]:
        load.start()

    barrier = pltpu.get_barrier_semaphore()
    for d in range(1, 8):
        pl.semaphore_signal(barrier, inc=1, device_id={"py": wrap(py + d, 8)}, device_id_type=MESH)
    for d in range(1, 16):
        pl.semaphore_signal(barrier, inc=1, device_id={"px": wrap(px + d, 16)}, device_id_type=MESH)

    def remote(src, dst, send, recv, axis, peer):
        return pltpu.make_async_remote_copy(
            src_ref=src, dst_ref=dst, send_sem=send, recv_sem=recv, device_id={axis: peer}, device_id_type=MESH
        )

    def send1(step, d, slot):
        part = pl.ds(channel_group(step) * 4, 4)
        peer = wrap(py + d, 8)
        return remote(z_out.at[peer, part], y_in.at[slot, part], s1.at[step, d], r1.at[step, d], "py", peer)

    def do_z(step):
        load_field(step).wait()
        group = channel_group(step)
        z_group(field, zt, z_out, group)
        y_in[py, pl.ds(group * 4, 4)] = z_out[py, pl.ds(group * 4, 4)]

    def send_z(step):
        for d in range(1, 8):
            send1(step, d, py).start()

    loads[0].wait()
    do_z(0)
    pl.semaphore_wait(barrier, 22)
    send_z(0)

    def z_step(step, carry):
        do_z(step)
        send_z(step)
        return carry

    lax.fori_loop(1, 8, z_step, 0)

    def send2(peer, slot, d):
        return remote(y_out.at[peer], x_in.at[slot], s2.at[d], r2.at[d], "px", peer)

    loads[1].wait()

    def y_step(step, carry):
        for d in range(1, 8):
            send1(step, d, wrap(py - d, 8)).wait_recv()
        group = channel_group(step)
        y_group(y_in, yt, y_out, y_rows, group)
        for half in range(2):
            peer = 2 * group + half

            @pl.when(peer != px)
            def _():
                send2(peer, px, wrap(peer - px, 16)).start()

        return carry

    lax.fori_loop(0, 8, y_step, 0)
    x_in[px] = y_out[px]
    for d in range(1, 16):
        send2(wrap(px + d, 16), wrap(px - d, 16), d).wait_recv()

    loads[2].wait()
    x_forward(x_in, xt, spec, px)
    loads[3].wait()

    def block(h, a, b):
        r, c = (b, a) if h == 0 else (a, b)
        return 4 * wrap(r, 4) + wrap(c, 4)

    near = [(col, row), (row, col)]
    steps = (0, -1, 1, 2)
    parts = (slice(0, 4), slice(0, 4), slice(0, 2), slice(2, 4))

    def first_phase(h, kind, receiving):
        a, b = near[h]
        sign = 1 if kind in (0, 2) else -1
        origin = (0, 0, -1, 1)[kind] - (sign if receiving else 0)
        place = spec.at[block(h, a + origin, b), h, parts[kind]]
        n = h * 20 + kind
        return remote(place, place, s3.at[n], r3.at[n], "px", block(h, a + sign, b))

    def second_phase(h, k, kind, receiving):
        a, b = near[h]
        sign = 1 if kind in (0, 2) else -1
        origin = (0, 0, -1, 1)[kind] - (sign if receiving else 0)
        place = spec.at[block(h, a + steps[k], b + origin), h, parts[kind]]
        n = h * 20 + 4 + 4 * k + kind
        return remote(place, place, s3.at[n], r3.at[n], "px", block(h, a, b + sign))

    def mix(h, da, db, fresh=False):
        a, b = near[h]
        mix_channel(spec, weight, sums, block(h, a + da, b + db), h, fresh)

    for h in range(2):
        for kind in range(2):
            first_phase(h, kind, False).start()
    for h in range(2):
        for kind in range(2):
            second_phase(h, 0, kind, False).start()
    mix(0, 0, 0, True)
    mix(1, 0, 0)
    for kind in range(2):
        for h in range(2):
            first_phase(h, kind, True).wait_recv()
            first_phase(h, kind + 2, False).start()
            for other in range(2):
                second_phase(h, kind + 1, other, False).start()
    for h in range(2):
        mix(h, -1, 0)
        mix(h, 1, 0)
    for h in range(2):
        for kind in (2, 3):
            first_phase(h, kind, True).wait_recv()
        for other in range(2):
            second_phase(h, 3, other, False).start()
    for h in range(2):
        mix(h, 2, 0)
    for k in range(4):
        for h in range(2):
            for kind in range(2):
                second_phase(h, k, kind, True).wait_recv()
                second_phase(h, k, kind + 2, False).start()
        for h in range(2):
            mix(h, steps[k], -1)
            mix(h, steps[k], 1)
    for k in range(4):
        for h in range(2):
            for kind in (2, 3):
                second_phase(h, k, kind, True).wait_recv()
            mix(h, steps[k], 2)

    loads[4].wait()
    x_inverse(sums, xit, m_out, m_rows)

    def send4(peer, slot, d):
        return remote(m_out.at[peer], b_in.at[slot], s4.at[d], r4.at[d], "px", peer)

    rows_order = (0, 1, 3, 2)
    for dr in rows_order:
        for dc in range(4):
            if dr or dc:
                peer = 4 * wrap(row - dr, 4) + wrap(col - dc, 4)
                send4(peer, px, 4 * dr + dc).start()
    b_in[px] = m_out[px]

    def send5(dr, d, slot):
        part = pl.ds(4 * wrap(row + dr, 4), 4)
        peer = wrap(py + d, 8)
        return remote(b_out.at[peer, part], out_hbm.at[slot, part], s5.at[dr, d], r5.at[dr, d], "py", peer)

    loads[5].wait()
    for dr in rows_order:
        for dc in range(4):
            if dr or dc:
                source = 4 * wrap(row + dr, 4) + wrap(col + dc, 4)
                send4(source, source, 4 * dr + dc).wait_recv()
        y_inverse(b_in, yit, b_out, wrap(row + dr, 4))
        for d in range(1, 8):
            send5(dr, d, py).start()
    own = pltpu.make_async_copy(b_out.at[py], out_hbm.at[py], own_sem)
    own.start()

    for dr in rows_order:
        for d in range(1, 8):
            send5(dr, d, wrap(py - d, 8)).wait_recv()
    own.wait()

    def drain(step, carry):
        for d in range(1, 8):
            send1(step, d, py).wait_send()
        return carry

    lax.fori_loop(0, 8, drain, 0)
    for d in range(1, 16):
        send2(wrap(px + d, 16), px, d).wait_send()
    for h in range(2):
        for kind in range(4):
            first_phase(h, kind, False).wait_send()
            for k in range(4):
                second_phase(h, k, kind, False).wait_send()
    for dr in range(4):
        for dc in range(4):
            if dr or dc:
                send4(4 * wrap(row - dr, 4) + wrap(col - dc, 4), px, 4 * dr + dc).wait_send()
        for d in range(1, 8):
            send5(dr, d, py).wait_send()


def finish(field_ref, spec_ref, point_ref, bias_ref, table_ref, out_ref, point_out, spread):
    @pl.when(pl.program_id(0) == 0)
    def _():
        r = lax.broadcasted_iota(jnp.int32, (256, 32), 0)
        c = lax.broadcasted_iota(jnp.int32, (256, 32), 1)
        tall = ((r >= 8 * c) & (r < 8 * c + 8)).astype(F32).astype(BF16)
        r = lax.broadcasted_iota(jnp.int32, (32, 256), 0)
        c = lax.broadcasted_iota(jnp.int32, (32, 256), 1)
        wide = ((c >= 8 * r) & (c < 8 * r + 8)).astype(F32).astype(BF16)
        r = lax.broadcasted_iota(jnp.int32, (256, 256), 0)
        c = lax.broadcasted_iota(jnp.int32, (256, 256), 1)
        every = dot(dot(tall, point_ref[...]).astype(BF16), wide)
        spread[...] = jnp.where((r & 7) == (c & 7), every, 0.0).astype(BF16)

    for x in range(4):
        for y in range(4):
            rows = field_ref[:, x, y * 8 : (y + 1) * 8, :].reshape(256, 256)
            point_out[:, x, y * 8 : (y + 1) * 8, :] = dot(spread[...], rows).reshape(32, 8, 256)

    def step(pair, carry):
        g = spec_ref[:, pair].reshape(128, 128)
        value = lax.dot_general(
            jnp.concatenate([g, g], axis=0),
            table_ref[...],
            (((0,), (0,)), ((), ())),
            preferred_element_type=F32,
        )
        for o in range(2):
            total = value[:, o * 256 : (o + 1) * 256].reshape(4, 32, 256) + point_out[2 * pair + o]
            total = total + bias_ref[2 * pair + o]
            total = 0.5 * total * (1.0 + lax.erf(total * 0.7071067811865476))
            out_ref[2 * pair + o] = total.astype(BF16)
        return carry

    lax.fori_loop(0, 16, step, 0)


def body(tables, field, spectral_weight, point_weight, point_bias):
    z_table, y_table, x_table, xi_table, yi_table, zi_table = tables
    field = field.reshape(32, 16, 32, 256)
    anywhere = pl.BlockSpec(memory_space=pl.ANY)
    dma = pltpu.SemaphoreType.DMA
    operands = (field, spectral_weight, z_table, y_table, x_table, xi_table, yi_table)
    spectral = pl.pallas_call(
        transform,
        out_shape=jax.ShapeDtypeStruct((8, 16, 2, 8, 512), BF16),
        in_specs=[anywhere] * len(operands),
        out_specs=anywhere,
        scratch_shapes=[
            *[pltpu.VMEM(a.shape, a.dtype) for a in operands],
            pltpu.VMEM((8, 32, 8, 512), BF16),
            pltpu.VMEM((8, 32, 8, 512), BF16),
            pltpu.VMEM((256, 128), F32),
            pltpu.VMEM((16, 2, 4, 16, 128), BF16),
            pltpu.VMEM((16, 2, 4, 16, 128), BF16),
            pltpu.VMEM((16, 2, 4, 64, 128), BF16),
            pltpu.VMEM((2, 4, 2, 64, 64), F32),
            pltpu.VMEM((2048, 128), F32),
            pltpu.VMEM((16, 128, 128), BF16),
            pltpu.VMEM((16, 128, 128), BF16),
            pltpu.VMEM((8, 16, 2, 8, 512), BF16),
            dma((6,)), dma((8,)),
            dma((8, 8)), dma((8, 8)),
            dma((16,)), dma((16,)),
            dma((40,)), dma((40,)),
            dma((16,)), dma((16,)),
            dma((4, 8)), dma((4, 8)),
            dma,
        ],
        compiler_params=pltpu.CompilerParams(
            collective_id=1, has_side_effects=True, vmem_limit_bytes=VMEM_LIMIT
        ),
        name="transform",
    )(*operands)
    out = pl.pallas_call(
        finish,
        grid=(4,),
        out_shape=jax.ShapeDtypeStruct((32, 16, 32, 256), BF16),
        in_specs=[
            pl.BlockSpec((32, 4, 32, 256), lambda x: (0, x, 0, 0)),
            pl.BlockSpec((8, 16, 2, 8, 128), lambda x: (0, 0, 0, 0, x)),
            pl.BlockSpec((32, 32), lambda x: (0, 0)),
            pl.BlockSpec(memory_space=pltpu.SMEM),
            pl.BlockSpec((256, 512), lambda x: (0, 0)),
        ],
        out_specs=pl.BlockSpec((32, 4, 32, 256), lambda x: (0, x, 0, 0)),
        scratch_shapes=[pltpu.VMEM((32, 4, 32, 256), F32), pltpu.VMEM((256, 256), BF16)],
        compiler_params=pltpu.CompilerParams(vmem_limit_bytes=VMEM_LIMIT),
        name="finish",
    )(field, spectral, point_weight, point_bias, zi_table)
    return out.reshape(1, 32, 16, 32, 256)


def solution(mesh):
    tables = tuple(jnp.asarray(t) for t in build_tables())

    def run(field, spectral_weight, point_weight, point_bias):
        return jax.shard_map(
            body,
            mesh=mesh,
            in_specs=((P(),) * 6, P(None, None, "px", "py", None), P(None, None, "px", "py", None, None), P(), P()),
            out_specs=P(None, None, "px", "py", None),
            check_vma=False,
        )(tables, field, spectral_weight, point_weight, point_bias)

    return run
```

time: 208 us -> 106 us (0.51)
  Pallas kernels: 202 us -> 106 us
  local copies, waits for them, and re-layouts: 4.96 us -> 0 us
    pallas_call x10 -> x1, Pallas kernels: 180 us -> 83.5 us  [body(): pl.pallas_call(transform, out_shape=jax.ShapeDtypeStruct((8, 16, 2, 8, 51...]
    convert_element_type x1 -> x0, local copies, waits for them, and re-layouts: 3.49 us -> none  [body(): jnp.kron(point_weight.astype(F32), jnp.eye(8, dtype=F32)).astype(BF16)]
where the time goes in v1:
time: 106 us
  Pallas kernels  106 us (100%)
    pallas_call x1, Pallas kernels, body(): pl.pallas_call(transform, out_shape=jax.ShapeDtypeStruct((8, 16, 2, 8, 51...  83.5 us
    pallas_call x1, Pallas kernels, body(): pl.pallas_call(finish, grid=(4,), out_shape=jax.ShapeDtypeStruct((32, 16,...  22.5 us

profile of v1, /device:TPU:1, one launch (start us, length us, event | category | flops | bytes accessed | tf_op | source)
XLA Modules:
  0.0 106.0 jit_solution(13898410631889041792)
XLA Ops:
  0.0 83.5 %transform.1.spec_ref = bf16[8,16,2,8,512]{4,3,2,1,0:T(8,128)(2,1)} custom-call(bf16[32,16,32,256]{3,2,1,0:T(8,128)(2,1)} %bitcast.2, bf16[2,32,2,4,64,64]{5,4,3,2,1,0:T(8,128)(2,1)} %weight_hbm.1, bf16[128,256]{1,0:T(8,128)(2,1)} %constant.12.clone.zt_hbm, bf16[1024,512]{1,0:T(8,128)(2,1)} %constant.13.clone.yt_hbm, ...), custom_call_target="tpu_custom_call" | custom-call | tf_op jit(solution)/shard_map/transform/pallas_call | solution.py:436
  83.5 22.5 %finish.1 = bf16[32,16,32,256]{3,2,1,0:T(8,128)(2,1)} custom-call(bf16[32,16,32,256]{3,2,1,0:T(8,128)(2,1)} %bitcast.3, bf16[8,16,2,8,512]{4,3,2,1,0:T(8,128)(2,1)} %transform.1.spec_ref, bf16[32,32]{1,0:T(8,128)(2,1)} %point_ref.1, f32[32]{0:T(128)} %bias_ref.1, bf16[256,512]{1,0:T(8,128)(2,1)} %constant.17.clone.table_ref), custom_call_target="tpu_custom_call" | custom-call | tf_op jit(solution)/shard_map/finish/pallas_call | solution.py:467

commit v2 on v1

--- a/solution.py
+++ b/solution.py
@@ -102,38 +102,33 @@
     first = lax.broadcasted_iota(jnp.int32, (128, 128), 1) < 64
     even = jnp.where(first, real, pltpu.roll(imag, 64, 1)).reshape(4, 4, 8, 128)
     odd = jnp.where(first, pltpu.roll(real, 64, 1), imag).reshape(4, 4, 8, 128)
-    out_ref[pl.ds(group * 2, 2)] = (
-        jnp.concatenate([even, odd], axis=2).astype(BF16).reshape(2, 2, 4, 16, 128)
-    )
-
-
-def x_forward(in_ref, table_ref, out_ref, me):
+    out_ref[group] = jnp.concatenate([even, odd], axis=2).astype(BF16).reshape(16, 16, 128)
+
+
+def x_group(in_ref, table_ref, out_ref, group, row, col):
+    both = dot(table_ref[...], in_ref[group].reshape(256, 128))
+    both = both[:128] + both[128:]
+    turned = pltpu.roll(both[64:], 64, 1)
     first = lax.broadcasted_iota(jnp.int32, (64, 128), 1) < 64
-    for c in range(2):
-        for l in range(4):
-            both = dot(table_ref[...], in_ref[:, c, l].reshape(256, 128))
-            both = both[:128] + both[128:]
-            turned = pltpu.roll(both[64:], 64, 1)
-            out_ref[me, c, l] = (both[:64] + jnp.where(first, turned, -turned)).astype(BF16)
-
-
-def mix_channel(spec_ref, weight_ref, sum_ref, p, h, fresh=False):
-    c = 2 * p + h
+    out_ref[group, row, col] = (both[:64] + jnp.where(first, turned, -turned)).astype(BF16)
+
+
+def mix_group(spec_ref, weight_ref, sum_ref, group):
     for l in range(4):
-        value = spec_ref[p, h, l].astype(F32)
-        real = value[:, :64]
-        imag = pltpu.roll(value, 64, 1)[:, :64]
+        sums = [None] * 4
+        for ci in range(4):
+            c = 4 * group + ci
+            value = spec_ref[group, ci, l].astype(F32)
+            real = value[:, :64]
+            imag = pltpu.roll(value, 64, 1)[:, :64]
+            for o in range(2):
+                wr = weight_ref[0, c, o, l].astype(F32)
+                wi = weight_ref[1, c, o, l].astype(F32)
+                for n, term in enumerate((real * wr - imag * wi, real * wi + imag * wr)):
+                    sums[2 * o + n] = term if ci == 0 else sums[2 * o + n] + term
         for o in range(2):
-            wr = weight_ref[0, c, o, l].astype(F32)
-            wi = weight_ref[1, c, o, l].astype(F32)
-            mr = real * wr - imag * wi
-            mi = real * wi + imag * wr
-            if fresh:
-                sum_ref[o, l, 0] = mr
-                sum_ref[o, l, 1] = mi
-            else:
-                sum_ref[o, l, 0] += mr
-                sum_ref[o, l, 1] += mi
+            for n in range(2):
+                sum_ref[o, l, n] += sums[2 * o + n]
 
 
 def x_inverse(sum_ref, table_ref, out_ref, rows_ref):
@@ -180,13 +175,8 @@
     def wrap(value, size):
         return lax.rem(value + size, size)
 
-    first_group = wrap(px // 2 + 1, 8)
-
-    def channel_group(step):
-        return wrap(first_group + step, 8)
-
     def load_field(step):
-        part = pl.ds(channel_group(step) * 4, 4)
+        part = pl.ds(step * 4, 4)
         return pltpu.make_async_copy(field_hbm.at[part], field.at[part], field_sem.at[step])
 
     loads = [
@@ -212,16 +202,18 @@
             src_ref=src, dst_ref=dst, send_sem=send, recv_sem=recv, device_id={axis: peer}, device_id_type=MESH
         )
 
+    def wait(view, semaphore):
+        pltpu.make_async_copy(view, view, semaphore).wait()
+
     def send1(step, d, slot):
-        part = pl.ds(channel_group(step) * 4, 4)
+        part = pl.ds(step * 4, 4)
         peer = wrap(py + d, 8)
-        return remote(z_out.at[peer, part], y_in.at[slot, part], s1.at[step, d], r1.at[step, d], "py", peer)
+        return remote(z_out.at[peer, part], y_in.at[slot, part], s1, r1.at[step], "py", peer)
 
     def do_z(step):
         load_field(step).wait()
-        group = channel_group(step)
-        z_group(field, zt, z_out, group)
-        y_in[py, pl.ds(group * 4, 4)] = z_out[py, pl.ds(group * 4, 4)]
+        z_group(field, zt, z_out, step)
+        y_in[py, pl.ds(step * 4, 4)] = z_out[py, pl.ds(step * 4, 4)]
 
     def send_z(step):
         for d in range(1, 8):
@@ -239,125 +231,90 @@
 
     lax.fori_loop(1, 8, z_step, 0)
 
-    def send2(peer, slot, d):
-        return remote(y_out.at[peer], x_in.at[slot], s2.at[d], r2.at[d], "px", peer)
+    def send2(step, peer, slot):
+        return remote(y_out.at[step, peer], x_in.at[step, slot], s2, r2.at[step], "px", peer)
+
+    def do_y(step):
+        wait(y_in.at[pl.ds(0, 7), pl.ds(step * 4, 4)], r1.at[step])
+        y_group(y_in, yt, y_out, y_rows, step)
+        for d in range(1, 16):
+            send2(step, wrap(px + d, 16), px).start()
+        x_in[step, px] = y_out[step, px]
+
+    halves = (pl.ds(0, 32), pl.ds(32, 32))
+
+    def gather(step, phase, h, d):
+        along_col = (h == 0) == (phase == 0)
+        if phase == 0:
+            place = spec.at[step, row, col, halves[h]]
+        elif along_col:
+            place = spec.at[step, :, col, halves[h]]
+        else:
+            place = spec.at[step, row, :, halves[h]]
+        peer = 4 * row + wrap(col + d, 4) if along_col else 4 * wrap(row + d, 4) + col
+        return remote(place, place, s3, r3.at[step, phase], "px", peer)
+
+    def do_x(step):
+        wait(x_in.at[step, pl.ds(0, 15)], r2.at[step])
+        x_group(x_in, xt, spec, step, row, col)
+        for d in (1, 3, 2):
+            for h in range(2):
+                gather(step, 0, h, d).start()
+
+    def do_second(step):
+        wait(spec.at[step, 0, pl.ds(0, 3)], r3.at[step, 0])
+        for h in range(2):
+            for d in (1, 3, 2):
+                gather(step, 1, h, d).start()
+
+    def do_mix(step):
+        wait(spec.at[step, pl.ds(0, 3)], r3.at[step, 1])
+        mix_group(spec, weight, sums, step)
 
     loads[1].wait()
+    loads[2].wait()
+    loads[3].wait()
+    sums[...] = jnp.zeros_like(sums)
 
     def y_step(step, carry):
-        for d in range(1, 8):
-            send1(step, d, wrap(py - d, 8)).wait_recv()
-        group = channel_group(step)
-        y_group(y_in, yt, y_out, y_rows, group)
-        for half in range(2):
-            peer = 2 * group + half
-
-            @pl.when(peer != px)
-            def _():
-                send2(peer, px, wrap(peer - px, 16)).start()
-
+        do_y(step)
+        pl.when(step >= 1)(lambda: do_x(step - 1))
+        pl.when(step >= 2)(lambda: do_second(step - 2))
+        pl.when(step >= 5)(lambda: do_mix(step - 5))
         return carry
 
     lax.fori_loop(0, 8, y_step, 0)
-    x_in[px] = y_out[px]
-    for d in range(1, 16):
-        send2(wrap(px + d, 16), wrap(px - d, 16), d).wait_recv()
-
-    loads[2].wait()
-    x_forward(x_in, xt, spec, px)
-    loads[3].wait()
-
-    def block(h, a, b):
-        r, c = (b, a) if h == 0 else (a, b)
-        return 4 * wrap(r, 4) + wrap(c, 4)
-
-    near = [(col, row), (row, col)]
-    steps = (0, -1, 1, 2)
-    parts = (slice(0, 4), slice(0, 4), slice(0, 2), slice(2, 4))
-
-    def first_phase(h, kind, receiving):
-        a, b = near[h]
-        sign = 1 if kind in (0, 2) else -1
-        origin = (0, 0, -1, 1)[kind] - (sign if receiving else 0)
-        place = spec.at[block(h, a + origin, b), h, parts[kind]]
-        n = h * 20 + kind
-        return remote(place, place, s3.at[n], r3.at[n], "px", block(h, a + sign, b))
-
-    def second_phase(h, k, kind, receiving):
-        a, b = near[h]
-        sign = 1 if kind in (0, 2) else -1
-        origin = (0, 0, -1, 1)[kind] - (sign if receiving else 0)
-        place = spec.at[block(h, a + steps[k], b + origin), h, parts[kind]]
-        n = h * 20 + 4 + 4 * k + kind
-        return remote(place, place, s3.at[n], r3.at[n], "px", block(h, a, b + sign))
-
-    def mix(h, da, db, fresh=False):
-        a, b = near[h]
-        mix_channel(spec, weight, sums, block(h, a + da, b + db), h, fresh)
-
-    for h in range(2):
-        for kind in range(2):
-            first_phase(h, kind, False).start()
-    for h in range(2):
-        for kind in range(2):
-            second_phase(h, 0, kind, False).start()
-    mix(0, 0, 0, True)
-    mix(1, 0, 0)
-    for kind in range(2):
-        for h in range(2):
-            first_phase(h, kind, True).wait_recv()
-            first_phase(h, kind + 2, False).start()
-            for other in range(2):
-                second_phase(h, kind + 1, other, False).start()
-    for h in range(2):
-        mix(h, -1, 0)
-        mix(h, 1, 0)
-    for h in range(2):
-        for kind in (2, 3):
-            first_phase(h, kind, True).wait_recv()
-        for other in range(2):
-            second_phase(h, 3, other, False).start()
-    for h in range(2):
-        mix(h, 2, 0)
-    for k in range(4):
-        for h in range(2):
-            for kind in range(2):
-                second_phase(h, k, kind, True).wait_recv()
-                second_phase(h, k, kind + 2, False).start()
-        for h in range(2):
-            mix(h, steps[k], -1)
-            mix(h, steps[k], 1)
-    for k in range(4):
-        for h in range(2):
-            for kind in (2, 3):
-                second_phase(h, k, kind, True).wait_recv()
-            mix(h, steps[k], 2)
+    do_mix(3)
+    do_x(7)
+    do_second(6)
+    do_mix(4)
+    do_mix(5)
+    do_second(7)
+    do_mix(6)
+    do_mix(7)
 
     loads[4].wait()
     x_inverse(sums, xit, m_out, m_rows)
 
     def send4(peer, slot, d):
-        return remote(m_out.at[peer], b_in.at[slot], s4.at[d], r4.at[d], "px", peer)
+        return remote(m_out.at[peer], b_in.at[slot], s4, r4.at[d], "px", peer)
 
     rows_order = (0, 1, 3, 2)
     for dr in rows_order:
         for dc in range(4):
             if dr or dc:
                 peer = 4 * wrap(row - dr, 4) + wrap(col - dc, 4)
-                send4(peer, px, 4 * dr + dc).start()
+                send4(peer, px, dr).start()
     b_in[px] = m_out[px]
 
     def send5(dr, d, slot):
         part = pl.ds(4 * wrap(row + dr, 4), 4)
         peer = wrap(py + d, 8)
-        return remote(b_out.at[peer, part], out_hbm.at[slot, part], s5.at[dr, d], r5.at[dr, d], "py", peer)
+        return remote(b_out.at[peer, part], out_hbm.at[slot, part], s5, r5.at[dr], "py", peer)
 
     loads[5].wait()
     for dr in rows_order:
-        for dc in range(4):
-            if dr or dc:
-                source = 4 * wrap(row + dr, 4) + wrap(col + dc, 4)
-                send4(source, source, 4 * dr + dc).wait_recv()
+        wait(b_in.at[pl.ds(0, 4 if dr else 3)], r4.at[dr])
         y_inverse(b_in, yit, b_out, wrap(row + dr, 4))
         for d in range(1, 8):
             send5(dr, d, py).start()
@@ -365,29 +322,15 @@
     own.start()
 
     for dr in rows_order:
-        for d in range(1, 8):
-            send5(dr, d, wrap(py - d, 8)).wait_recv()
+        wait(out_hbm.at[pl.ds(0, 7), pl.ds(4 * dr, 4)], r5.at[dr])
     own.wait()
 
-    def drain(step, carry):
-        for d in range(1, 8):
-            send1(step, d, py).wait_send()
-        return carry
-
-    lax.fori_loop(0, 8, drain, 0)
-    for d in range(1, 16):
-        send2(wrap(px + d, 16), px, d).wait_send()
-    for h in range(2):
-        for kind in range(4):
-            first_phase(h, kind, False).wait_send()
-            for k in range(4):
-                second_phase(h, k, kind, False).wait_send()
-    for dr in range(4):
-        for dc in range(4):
-            if dr or dc:
-                send4(4 * wrap(row - dr, 4) + wrap(col - dc, 4), px, 4 * dr + dc).wait_send()
-        for d in range(1, 8):
-            send5(dr, d, py).wait_send()
+    wait(z_out.at[pl.ds(0, 7)], s1)
+    wait(y_out.at[:, pl.ds(0, 15)], s2)
+    wait(spec.at[:, 0, pl.ds(0, 3)], s3)
+    wait(spec.at[:, pl.ds(0, 3)], s3)
+    wait(m_out.at[pl.ds(0, 15)], s4)
+    wait(b_out.at[pl.ds(0, 7)], s5)
 
 
 def finish(field_ref, spec_ref, point_ref, bias_ref, table_ref, out_ref, point_out, spread):
@@ -424,7 +367,7 @@
             out_ref[2 * pair + o] = total.astype(BF16)
         return carry
 
-    lax.fori_loop(0, 16, step, 0)
+    lax.fori_loop(0, 16, step, 0, unroll=8)
 
 
 def body(tables, field, spectral_weight, point_weight, point_bias):
@@ -443,20 +386,20 @@
             pltpu.VMEM((8, 32, 8, 512), BF16),
             pltpu.VMEM((8, 32, 8, 512), BF16),
             pltpu.VMEM((256, 128), F32),
-            pltpu.VMEM((16, 2, 4, 16, 128), BF16),
-            pltpu.VMEM((16, 2, 4, 16, 128), BF16),
-            pltpu.VMEM((16, 2, 4, 64, 128), BF16),
+            pltpu.VMEM((8, 16, 16, 128), BF16),
+            pltpu.VMEM((8, 16, 16, 128), BF16),
+            pltpu.VMEM((8, 4, 4, 64, 128), BF16),
             pltpu.VMEM((2, 4, 2, 64, 64), F32),
             pltpu.VMEM((2048, 128), F32),
             pltpu.VMEM((16, 128, 128), BF16),
             pltpu.VMEM((16, 128, 128), BF16),
             pltpu.VMEM((8, 16, 2, 8, 512), BF16),
             dma((6,)), dma((8,)),
-            dma((8, 8)), dma((8, 8)),
-            dma((16,)), dma((16,)),
-            dma((40,)), dma((40,)),
-            dma((16,)), dma((16,)),
-            dma((4, 8)), dma((4, 8)),
+            dma, dma((8,)),
+            dma, dma((8,)),
+            dma, dma((8, 2)),
+            dma, dma((4,)),
+            dma, dma((4,)),
             dma,
         ],
         compiler_params=pltpu.CompilerParams(

time: 106 us -> 89.6 us (0.85)
  Pallas kernels: 106 us -> 89.4 us
    pallas_call x1, Pallas kernels: 22.5 us -> 12.5 us  [body(): pl.pallas_call(finish, grid=(4,), out_shape=jax.ShapeDtypeStruct((32, 16,...]
    pallas_call x1, Pallas kernels: 83.5 us -> 76.8 us  [body(): pl.pallas_call(transform, out_shape=jax.ShapeDtypeStruct((8, 16, 2, 8, 51...]
where the time goes in v2:
time: 89.6 us; the launch traced here: 89.4 us
  Pallas kernels  89.4 us (100%)
    pallas_call x1, Pallas kernels, body(): pl.pallas_call(transform, out_shape=jax.ShapeDtypeStruct((8, 16, 2, 8, 51...  76.8 us
    pallas_call x1, Pallas kernels, body(): pl.pallas_call(finish, grid=(4,), out_shape=jax.ShapeDtypeStruct((32, 16,...  12.5 us

profile of v2, /device:TPU:1, one launch (start us, length us, event | category | flops | bytes accessed | tf_op | source)
XLA Modules:
  0.0 89.4 jit_solution(5269614895150434699)
XLA Ops:
  0.0 76.8 %transform.1.spec_ref = bf16[8,16,2,8,512]{4,3,2,1,0:T(8,128)(2,1)} custom-call(bf16[32,16,32,256]{3,2,1,0:T(8,128)(2,1)} %bitcast.2, bf16[2,32,2,4,64,64]{5,4,3,2,1,0:T(8,128)(2,1)} %weight_hbm.1, bf16[128,256]{1,0:T(8,128)(2,1)} %constant.12.clone.zt_hbm, bf16[1024,512]{1,0:T(8,128)(2,1)} %constant.13.clone.yt_hbm, ...), custom_call_target="tpu_custom_call" | custom-call | tf_op jit(solution)/shard_map/transform/pallas_call | solution.py:379
  76.9 12.5 %finish.1 = bf16[32,16,32,256]{3,2,1,0:T(8,128)(2,1)} custom-call(bf16[32,16,32,256]{3,2,1,0:T(8,128)(2,1)} %bitcast.3, bf16[8,16,2,8,512]{4,3,2,1,0:T(8,128)(2,1)} %transform.1.spec_ref, bf16[32,32]{1,0:T(8,128)(2,1)} %point_ref.1, f32[32]{0:T(128)} %bias_ref.1, bf16[256,512]{1,0:T(8,128)(2,1)} %constant.17.clone.table_ref), custom_call_target="tpu_custom_call" | custom-call | tf_op jit(solution)/shard_map/finish/pallas_call | solution.py:410

commit v3 on v2

--- a/solution.py
+++ b/solution.py
@@ -161,11 +161,44 @@
                 out_ref[q, part, ri, :, quad * 128 : (quad + 1) * 128] = value[quad, :, :, q * 128 : (q + 1) * 128]
 
 
+def spread_point(point, spread):
+    r = lax.broadcasted_iota(jnp.int32, (256, 32), 0)
+    c = lax.broadcasted_iota(jnp.int32, (256, 32), 1)
+    tall = ((r >= 8 * c) & (r < 8 * c + 8)).astype(F32).astype(BF16)
+    r = lax.broadcasted_iota(jnp.int32, (32, 256), 0)
+    c = lax.broadcasted_iota(jnp.int32, (32, 256), 1)
+    wide = ((c >= 8 * r) & (c < 8 * r + 8)).astype(F32).astype(BF16)
+    r = lax.broadcasted_iota(jnp.int32, (256, 256), 0)
+    c = lax.broadcasted_iota(jnp.int32, (256, 256), 1)
+    every = dot(dot(tall, point[...]).astype(BF16), wide)
+    spread[...] = jnp.where((r & 7) == (c & 7), every, 0.0).astype(BF16)
+
+
+def point_plane(field_ref, spread, out_ref, x):
+    for y in range(4):
+        rows = field_ref[:, x, y * 8 : (y + 1) * 8, :].reshape(256, 256)
+        out_ref[:, x, y * 8 : (y + 1) * 8, :] = dot(spread[...], rows).reshape(32, 8, 256)
+
+
+def activate(g, point_rows, bias, table_ref):
+    value = lax.dot_general(
+        jnp.concatenate([g, g], axis=0), table_ref[...], (((0,), (0,)), ((), ())), preferred_element_type=F32
+    )
+    out = []
+    for o in range(2):
+        total = value[:, o * 256 : (o + 1) * 256].reshape(4, 32, 256) + point_rows[o]
+        total = total + bias[o]
+        out.append((0.5 * total * (1.0 + lax.erf(total * 0.7071067811865476))).astype(BF16))
+    return out
+
+
 def transform(
-    field_hbm, weight_hbm, zt_hbm, yt_hbm, xt_hbm, xit_hbm, yit_hbm, out_hbm,
-    field, weight, zt, yt, xt, xit, yit,
+    field_hbm, weight_hbm, zt_hbm, yt_hbm, xt_hbm, xit_hbm, yit_hbm, zit_hbm, point_hbm, bias_hbm,
+    out_hbm, late_hbm, plane_hbm,
+    field, weight, zt, yt, xt, xit, yit, zit, point, bias,
     z_out, y_in, y_rows, y_out, x_in, spec, sums, m_rows, m_out, b_in, b_out,
-    load_sem, field_sem, s1, r1, s2, r2, s3, r3, s4, r4, s5, r5, own_sem,
+    spread, planes, f_in, stage,
+    load_sem, field_sem, s1, r1, s2, r2, s3, r3, s4, r4, s5, r5, own_sem, out_sem,
 ):
     px = lax.axis_index("px")
     py = lax.axis_index("py")
@@ -182,7 +215,8 @@
     loads = [
         pltpu.make_async_copy(a, b, load_sem.at[n])
         for n, (a, b) in enumerate(
-            ((zt_hbm, zt), (yt_hbm, yt), (xt_hbm, xt), (weight_hbm, weight), (xit_hbm, xit), (yit_hbm, yit))
+            ((zt_hbm, zt), (yt_hbm, yt), (xt_hbm, xt), (weight_hbm, weight), (xit_hbm, xit), (yit_hbm, yit),
+             (zit_hbm, zit), (point_hbm, point), (bias_hbm, bias))
         )
     ]
     loads[0].start()
@@ -275,9 +309,13 @@
     loads[2].wait()
     loads[3].wait()
     sums[...] = jnp.zeros_like(sums)
+    loads[7].wait()
+    spread_point(point, spread)
 
     def y_step(step, carry):
         do_y(step)
+        point_plane(field, spread, planes, 2 * step)
+        point_plane(field, spread, planes, 2 * step + 1)
         pl.when(step >= 1)(lambda: do_x(step - 1))
         pl.when(step >= 2)(lambda: do_second(step - 2))
         pl.when(step >= 5)(lambda: do_mix(step - 5))
@@ -307,23 +345,58 @@
                 send4(peer, px, dr).start()
     b_in[px] = m_out[px]
 
-    def send5(dr, d, slot):
+    last = 2
+    late = pl.ds(8 * wrap(row + last, 4), 8)
+    spare = pltpu.make_async_copy(planes.at[late], plane_hbm, own_sem.at[0])
+    spare.start()
+
+    def send5(dr, d):
         part = pl.ds(4 * wrap(row + dr, 4), 4)
         peer = wrap(py + d, 8)
-        return remote(b_out.at[peer, part], out_hbm.at[slot, part], s5, r5.at[dr], "py", peer)
+        place = late_hbm.at[py] if dr == last else f_in.at[py, part]
+        return remote(b_out.at[peer, part], place, s5, r5.at[dr], "py", peer)
 
     loads[5].wait()
     for dr in rows_order:
         wait(b_in.at[pl.ds(0, 4 if dr else 3)], r4.at[dr])
+        part = pl.ds(4 * wrap(row + dr, 4), 4)
         y_inverse(b_in, yit, b_out, wrap(row + dr, 4))
         for d in range(1, 8):
-            send5(dr, d, py).start()
-    own = pltpu.make_async_copy(b_out.at[py], out_hbm.at[py], own_sem)
-    own.start()
-
-    for dr in rows_order:
-        wait(out_hbm.at[pl.ds(0, 7), pl.ds(4 * dr, 4)], r5.at[dr])
+            send5(dr, d).start()
+        if dr == last:
+            own = pltpu.make_async_copy(b_out.at[py, part], late_hbm.at[py], own_sem.at[1])
+            own.start()
+        else:
+            f_in[py, part] = b_out[py, part]
+
+    loads[6].wait()
+    loads[8].wait()
+    stores = []
+    for n, dr in enumerate(rows_order[:3]):
+        group = wrap(row + dr, 4)
+        wait(f_in.at[pl.ds(0, 7), pl.ds(0, 4)], r5.at[dr])
+
+        def final(pair, carry, n=n, group=group):
+            op = 4 * group + pair
+            for quad in range(4):
+                g = f_in[:, op, :, :, quad * 128 : (quad + 1) * 128].reshape(128, 128)
+                part = slice(4 * quad, 4 * quad + 4)
+                done = activate(
+                    g, [planes[2 * op + o, part] for o in range(2)], [bias[2 * op + o] for o in range(2)], zit
+                )
+                for o in range(2):
+                    stage[n, 2 * pair + o, part] = done[o]
+            return carry
+
+        lax.fori_loop(0, 4, final, 0, unroll=2)
+        store = pltpu.make_async_copy(stage.at[n], out_hbm.at[pl.ds(8 * group, 8)], out_sem.at[n])
+        store.start()
+        stores.append(store)
+    wait(late_hbm.at[pl.ds(0, 7)], r5.at[last])
+    spare.wait()
     own.wait()
+    for store in stores:
+        store.wait()
 
     wait(z_out.at[pl.ds(0, 7)], s1)
     wait(y_out.at[:, pl.ds(0, 15)], s2)
@@ -333,41 +406,59 @@
     wait(b_out.at[pl.ds(0, 7)], s5)
 
 
-def finish(field_ref, spec_ref, point_ref, bias_ref, table_ref, out_ref, point_out, spread):
-    @pl.when(pl.program_id(0) == 0)
-    def _():
-        r = lax.broadcasted_iota(jnp.int32, (256, 32), 0)
-        c = lax.broadcasted_iota(jnp.int32, (256, 32), 1)
-        tall = ((r >= 8 * c) & (r < 8 * c + 8)).astype(F32).astype(BF16)
-        r = lax.broadcasted_iota(jnp.int32, (32, 256), 0)
-        c = lax.broadcasted_iota(jnp.int32, (32, 256), 1)
-        wide = ((c >= 8 * r) & (c < 8 * r + 8)).astype(F32).astype(BF16)
-        r = lax.broadcasted_iota(jnp.int32, (256, 256), 0)
-        c = lax.broadcasted_iota(jnp.int32, (256, 256), 1)
-        every = dot(dot(tall, point_ref[...]).astype(BF16), wide)
-        spread[...] = jnp.where((r & 7) == (c & 7), every, 0.0).astype(BF16)
-
-    for x in range(4):
-        for y in range(4):
-            rows = field_ref[:, x, y * 8 : (y + 1) * 8, :].reshape(256, 256)
-            point_out[:, x, y * 8 : (y + 1) * 8, :] = dot(spread[...], rows).reshape(32, 8, 256)
-
-    def step(pair, carry):
-        g = spec_ref[:, pair].reshape(128, 128)
-        value = lax.dot_general(
-            jnp.concatenate([g, g], axis=0),
-            table_ref[...],
-            (((0,), (0,)), ((), ())),
-            preferred_element_type=F32,
-        )
-        for o in range(2):
-            total = value[:, o * 256 : (o + 1) * 256].reshape(4, 32, 256) + point_out[2 * pair + o]
-            total = total + bias_ref[2 * pair + o]
-            total = 0.5 * total * (1.0 + lax.erf(total * 0.7071067811865476))
-            out_ref[2 * pair + o] = total.astype(BF16)
-        return carry
-
-    lax.fori_loop(0, 16, step, 0, unroll=8)
+def finish(early_hbm, late_hbm, plane_hbm, bias, zit_hbm, out_hbm, late, planes, zit, stage, held, sems):
+    row = lax.axis_index("px") // 4
+    group = lax.rem(row + 2, 4)
+
+    def load_plane(quad):
+        part = pl.ds(4 * quad, 4)
+        return pltpu.make_async_copy(plane_hbm.at[:, part], planes.at[:, part], sems.at[quad])
+
+    def store(quad):
+        part = pl.ds(4 * quad, 4)
+        return pltpu.make_async_copy(stage.at[:, part], out_hbm.at[pl.ds(8 * group, 8), part], sems.at[4 + quad])
+
+    def through(n, j, inward):
+        part = pl.ds(8 * lax.rem(row + (0, 1, 3)[n], 4) + 4 * j, 4)
+        if inward:
+            return pltpu.make_async_copy(early_hbm.at[part], held.at[n, j], sems.at[10 + 2 * n + j])
+        return pltpu.make_async_copy(held.at[n, j], out_hbm.at[part], sems.at[16 + 2 * n + j])
+
+    chunks = [(n, j) for n in range(3) for j in range(2)]
+    first = [
+        pltpu.make_async_copy(zit_hbm, zit, sems.at[8]),
+        pltpu.make_async_copy(late_hbm, late, sems.at[9]),
+    ]
+    for copy in first:
+        copy.start()
+    for quad in range(4):
+        load_plane(quad).start()
+        if quad == 0:
+            for n, j in chunks:
+                through(n, j, True).start()
+    for copy in first:
+        copy.wait()
+    for quad in range(4):
+        load_plane(quad).wait()
+        part = slice(4 * quad, 4 * quad + 4)
+        for pair in range(4):
+            g = late[:, pair, :, :, quad * 128 : (quad + 1) * 128].reshape(128, 128)
+            done = activate(
+                g,
+                [planes[2 * pair + o, part] for o in range(2)],
+                [bias[8 * group + 2 * pair + o] for o in range(2)],
+                zit,
+            )
+            for o in range(2):
+                stage[2 * pair + o, part] = done[o]
+        store(quad).start()
+        for n, j in chunks[2 * quad : 2 * quad + 2]:
+            through(n, j, True).wait()
+            through(n, j, False).start()
+    for quad in range(4):
+        store(quad).wait()
+    for n, j in chunks:
+        through(n, j, False).wait()
 
 
 def body(tables, field, spectral_weight, point_weight, point_bias):
@@ -375,14 +466,19 @@
     field = field.reshape(32, 16, 32, 256)
     anywhere = pl.BlockSpec(memory_space=pl.ANY)
     dma = pltpu.SemaphoreType.DMA
-    operands = (field, spectral_weight, z_table, y_table, x_table, xi_table, yi_table)
-    spectral = pl.pallas_call(
+    operands = (field, spectral_weight, z_table, y_table, x_table, xi_table, yi_table, zi_table, point_weight)
+    early, late, planes = pl.pallas_call(
         transform,
-        out_shape=jax.ShapeDtypeStruct((8, 16, 2, 8, 512), BF16),
-        in_specs=[anywhere] * len(operands),
-        out_specs=anywhere,
+        out_shape=(
+            jax.ShapeDtypeStruct((32, 16, 32, 256), BF16),
+            jax.ShapeDtypeStruct((8, 4, 2, 8, 512), BF16),
+            jax.ShapeDtypeStruct((8, 16, 32, 256), F32),
+        ),
+        in_specs=[anywhere] * (len(operands) + 1),
+        out_specs=(anywhere,) * 3,
         scratch_shapes=[
             *[pltpu.VMEM(a.shape, a.dtype) for a in operands],
+            pltpu.SMEM((32,), F32),
             pltpu.VMEM((8, 32, 8, 512), BF16),
             pltpu.VMEM((8, 32, 8, 512), BF16),
             pltpu.VMEM((256, 128), F32),
@@ -394,35 +490,39 @@
             pltpu.VMEM((16, 128, 128), BF16),
             pltpu.VMEM((16, 128, 128), BF16),
             pltpu.VMEM((8, 16, 2, 8, 512), BF16),
-            dma((6,)), dma((8,)),
+            pltpu.VMEM((256, 256), BF16),
+            pltpu.VMEM((32, 16, 32, 256), F32),
+            pltpu.VMEM((8, 16, 2, 8, 512), BF16),
+            pltpu.VMEM((3, 8, 16, 32, 256), BF16),
+            dma((9,)), dma((8,)),
             dma, dma((8,)),
             dma, dma((8,)),
             dma, dma((8, 2)),
             dma, dma((4,)),
             dma, dma((4,)),
-            dma,
+            dma((2,)), dma((3,)),
         ],
         compiler_params=pltpu.CompilerParams(
             collective_id=1, has_side_effects=True, vmem_limit_bytes=VMEM_LIMIT
         ),
         name="transform",
-    )(*operands)
+    )(*operands, point_bias)
     out = pl.pallas_call(
         finish,
-        grid=(4,),
         out_shape=jax.ShapeDtypeStruct((32, 16, 32, 256), BF16),
-        in_specs=[
-            pl.BlockSpec((32, 4, 32, 256), lambda x: (0, x, 0, 0)),
-            pl.BlockSpec((8, 16, 2, 8, 128), lambda x: (0, 0, 0, 0, x)),
-            pl.BlockSpec((32, 32), lambda x: (0, 0)),
-            pl.BlockSpec(memory_space=pltpu.SMEM),
-            pl.BlockSpec((256, 512), lambda x: (0, 0)),
+        in_specs=[anywhere] * 3 + [pl.BlockSpec(memory_space=pltpu.SMEM), anywhere],
+        out_specs=anywhere,
+        scratch_shapes=[
+            pltpu.VMEM((8, 4, 2, 8, 512), BF16),
+            pltpu.VMEM((8, 16, 32, 256), F32),
+            pltpu.VMEM((256, 512), BF16),
+            pltpu.VMEM((8, 16, 32, 256), BF16),
+            pltpu.VMEM((3, 2, 4, 16, 32, 256), BF16),
+            dma((22,)),
         ],
-        out_specs=pl.BlockSpec((32, 4, 32, 256), lambda x: (0, x, 0, 0)),
-        scratch_shapes=[pltpu.VMEM((32, 4, 32, 256), F32), pltpu.VMEM((256, 256), BF16)],
         compiler_params=pltpu.CompilerParams(vmem_limit_bytes=VMEM_LIMIT),
         name="finish",
-    )(field, spectral, point_weight, point_bias, zi_table)
+    )(early, late, planes, point_bias, zi_table)
     return out.reshape(1, 32, 16, 32, 256)
 
 

time: 89.6 us -> 85.2 us (0.951)
  Pallas kernels: 89.4 us -> 85.1 us
    pallas_call x2, Pallas kernels: 89.4 us -> 85.1 us  [the longest x1 76.7 us: body(): pl.pallas_call(transform, out_shape=(jax.ShapeDtypeStruct((32, 16, 32, 25...]
where the time goes in v3:
time: 85.2 us; the launch traced here: 85.1 us
  Pallas kernels  85.1 us (100%)
    pallas_call x1, Pallas kernels, body(): pl.pallas_call(transform, out_shape=(jax.ShapeDtypeStruct((32, 16, 32, 25...  76.7 us
    pallas_call x1, Pallas kernels, body(): pl.pallas_call(finish, out_shape=jax.ShapeDtypeStruct((32, 16, 32, 256),...  8.39 us

profile of v3, /device:TPU:1, one launch (start us, length us, event | category | flops | bytes accessed | tf_op | source)
XLA Modules:
  0.0 85.1 jit_solution(16832172327050346574)
XLA Ops:
  0.0 76.7 %transform.1 = (bf16[32,16,32,256]{3,2,1,0:T(8,128)(2,1)}, bf16[8,4,2,8,512]{4,3,2,1,0:T(8,128)(2,1)}, f32[8,16,32,256]{3,2,1,0:T(8,128)}) custom-call(bf16[32,16,32,256]{3,2,1,0:T(8,128)(2,1)} %bitcast.2, bf16[2,32,2,4,64,64]{5,4,3,2,1,0:T(8,128)(2,1)} %weight_hbm.1, bf16[128,256]{1,0:T(8,128)(2,1)} %constant.12.clone.zt_hbm, ...), custom_call_target="tpu_custom_call" | custom-call | tf_op jit(solution)/shard_map/transform/pallas_call | solution.py:470
  76.7 8.4 %finish.1 = bf16[32,16,32,256]{3,2,1,0:T(8,128)(2,1)} custom-call(bf16[32,16,32,256]{3,2,1,0:T(8,128)(2,1)} %get-tuple-element.8.early_hbm, bf16[8,4,2,8,512]{4,3,2,1,0:T(8,128)(2,1)} %get-tuple-element.9.late_hbm, f32[8,16,32,256]{3,2,1,0:T(8,128)} %get-tuple-element.10.plane_hbm, f32[32]{0:T(128)} %bias.1, bf16[256,512]{1,0:T(8,128)(2,1)} %constant.17.clone.zit_hbm), custom_call_target="tpu_custom_call" | custom-call | tf_op jit(solution)/shard_map/finish/pallas_call | solution.py:510

commit v4 on v3

--- a/solution.py
+++ b/solution.py
@@ -12,7 +12,7 @@
 F32 = jnp.float32
 BF16 = jnp.bfloat16
 MESH = pl.DeviceIdType.MESH
-VMEM_LIMIT = 60 * 1024 * 1024
+VMEM_LIMIT = 62 * 1024 * 1024
 
 
 def split_bf16(table):
@@ -197,8 +197,8 @@
     out_hbm, late_hbm, plane_hbm,
     field, weight, zt, yt, xt, xit, yit, zit, point, bias,
     z_out, y_in, y_rows, y_out, x_in, spec, sums, m_rows, m_out, b_in, b_out,
-    spread, planes, f_in, stage,
-    load_sem, field_sem, s1, r1, s2, r2, s3, r3, s4, r4, s5, r5, own_sem, out_sem,
+    spread, planes, narrow, f_in, stage,
+    load_sem, field_sem, s1, r1, s2, r2, s3, r3, s4, r4, s5, r5, own_sem, out_sem, r6,
 ):
     px = lax.axis_index("px")
     py = lax.axis_index("py")
@@ -288,9 +288,14 @@
         peer = 4 * row + wrap(col + d, 4) if along_col else 4 * wrap(row + d, 4) + col
         return remote(place, place, s3, r3.at[step, phase], "px", peer)
 
-    def do_x(step):
+    def do_x(step, direct=False):
         wait(x_in.at[step, pl.ds(0, 15)], r2.at[step])
         x_group(x_in, xt, spec, step, row, col)
+        if direct:
+            place = spec.at[step, row, col]
+            for d in range(1, 16):
+                remote(place, place, s3, r6, "px", wrap(px + d, 16)).start()
+            return
         for d in (1, 3, 2):
             for h in range(2):
                 gather(step, 0, h, d).start()
@@ -301,8 +306,11 @@
             for d in (1, 3, 2):
                 gather(step, 1, h, d).start()
 
-    def do_mix(step):
-        wait(spec.at[step, pl.ds(0, 3)], r3.at[step, 1])
+    def do_mix(step, direct=False):
+        if direct:
+            wait(spec.at[pl.ds(0, 5), pl.ds(0, 3), 0], r6)
+        else:
+            wait(spec.at[step, pl.ds(0, 3)], r3.at[step, 1])
         mix_group(spec, weight, sums, step)
 
     loads[1].wait()
@@ -316,20 +324,22 @@
         do_y(step)
         point_plane(field, spread, planes, 2 * step)
         point_plane(field, spread, planes, 2 * step + 1)
-        pl.when(step >= 1)(lambda: do_x(step - 1))
-        pl.when(step >= 2)(lambda: do_second(step - 2))
-        pl.when(step >= 5)(lambda: do_mix(step - 5))
+        pl.when(step >= 2)(lambda: do_x(step - 2))
+        pl.when(step >= 3)(lambda: do_second(step - 3))
+        pl.when(step >= 6)(lambda: do_mix(step - 6))
         return carry
 
     lax.fori_loop(0, 8, y_step, 0)
+    do_x(6)
+    do_second(5)
+    do_mix(2)
+    do_x(7, True)
+    do_second(6)
     do_mix(3)
-    do_x(7)
-    do_second(6)
     do_mix(4)
     do_mix(5)
-    do_second(7)
     do_mix(6)
-    do_mix(7)
+    do_mix(7, True)
 
     loads[4].wait()
     x_inverse(sums, xit, m_out, m_rows)
@@ -347,7 +357,8 @@
 
     last = 2
     late = pl.ds(8 * wrap(row + last, 4), 8)
-    spare = pltpu.make_async_copy(planes.at[late], plane_hbm, own_sem.at[0])
+    narrow[...] = planes[late].astype(BF16)
+    spare = pltpu.make_async_copy(narrow, plane_hbm, own_sem.at[0])
     spare.start()
 
     def send5(dr, d):
@@ -445,7 +456,7 @@
             g = late[:, pair, :, :, quad * 128 : (quad + 1) * 128].reshape(128, 128)
             done = activate(
                 g,
-                [planes[2 * pair + o, part] for o in range(2)],
+                [planes[2 * pair + o, part].astype(F32) for o in range(2)],
                 [bias[8 * group + 2 * pair + o] for o in range(2)],
                 zit,
             )
@@ -472,7 +483,7 @@
         out_shape=(
             jax.ShapeDtypeStruct((32, 16, 32, 256), BF16),
             jax.ShapeDtypeStruct((8, 4, 2, 8, 512), BF16),
-            jax.ShapeDtypeStruct((8, 16, 32, 256), F32),
+            jax.ShapeDtypeStruct((8, 16, 32, 256), BF16),
         ),
         in_specs=[anywhere] * (len(operands) + 1),
         out_specs=(anywhere,) * 3,
@@ -492,6 +503,7 @@
             pltpu.VMEM((8, 16, 2, 8, 512), BF16),
             pltpu.VMEM((256, 256), BF16),
             pltpu.VMEM((32, 16, 32, 256), F32),
+            pltpu.VMEM((8, 16, 32, 256), BF16),
             pltpu.VMEM((8, 16, 2, 8, 512), BF16),
             pltpu.VMEM((3, 8, 16, 32, 256), BF16),
             dma((9,)), dma((8,)),
@@ -500,7 +512,7 @@
             dma, dma((8, 2)),
             dma, dma((4,)),
             dma, dma((4,)),
-            dma((2,)), dma((3,)),
+            dma((2,)), dma((3,)), dma,
         ],
         compiler_params=pltpu.CompilerParams(
             collective_id=1, has_side_effects=True, vmem_limit_bytes=VMEM_LIMIT
@@ -514,7 +526,7 @@
         out_specs=anywhere,
         scratch_shapes=[
             pltpu.VMEM((8, 4, 2, 8, 512), BF16),
-            pltpu.VMEM((8, 16, 32, 256), F32),
+            pltpu.VMEM((8, 16, 32, 256), BF16),
             pltpu.VMEM((256, 512), BF16),
             pltpu.VMEM((8, 16, 32, 256), BF16),
             pltpu.VMEM((3, 2, 4, 16, 32, 256), BF16),

time: 85.2 us -> 86.4 us (1.014); the launches traced: 85.1 us -> 84.8 us
  no operation moved by 1% of the time
where the time goes in v4:
time: 86.4 us; the launch traced here: 84.8 us
  Pallas kernels  84.8 us (98%)
    pallas_call x1, Pallas kernels, body(): pl.pallas_call(transform, out_shape=(jax.ShapeDtypeStruct((32, 16, 32, 25...  76.7 us
    pallas_call x1, Pallas kernels, body(): pl.pallas_call(finish, out_shape=jax.ShapeDtypeStruct((32, 16, 32, 256),...  8.08 us

profile of v4, /device:TPU:1, one launch (start us, length us, event | category | flops | bytes accessed | tf_op | source)
XLA Modules:
  0.0 84.8 jit_solution(10695280048777304692)
XLA Ops:
  0.0 76.7 %transform.1 = (bf16[32,16,32,256]{3,2,1,0:T(8,128)(2,1)}, bf16[8,4,2,8,512]{4,3,2,1,0:T(8,128)(2,1)}, bf16[8,16,32,256]{3,2,1,0:T(8,128)(2,1)}) custom-call(bf16[32,16,32,256]{3,2,1,0:T(8,128)(2,1)} %bitcast.2, bf16[2,32,2,4,64,64]{5,4,3,2,1,0:T(8,128)(2,1)} %weight_hbm.1, bf16[128,256]{1,0:T(8,128)(2,1)} %constant.12.clone.zt_hbm, ...), custom_call_target="tpu_custom_call" | custom-call | tf_op jit(solution)/shard_map/transform/pallas_call | solution.py:481
  76.7 8.1 %finish.1 = bf16[32,16,32,256]{3,2,1,0:T(8,128)(2,1)} custom-call(bf16[32,16,32,256]{3,2,1,0:T(8,128)(2,1)} %get-tuple-element.8.early_hbm, bf16[8,4,2,8,512]{4,3,2,1,0:T(8,128)(2,1)} %get-tuple-element.9.late_hbm, bf16[8,16,32,256]{3,2,1,0:T(8,128)(2,1)} %get-tuple-element.10.plane_hbm, f32[32]{0:T(128)} %bias.1, bf16[256,512]{1,0:T(8,128)(2,1)} %constant.17.clone.zit_hbm), custom_call_target="tpu_custom_call" | custom-call | tf_op jit(solution)/shard_map/finish/pallas_call | solution.py:522

commit v5 on v3

--- a/solution.py
+++ b/solution.py
@@ -347,7 +347,8 @@
 
     last = 2
     late = pl.ds(8 * wrap(row + last, 4), 8)
-    spare = pltpu.make_async_copy(planes.at[late], plane_hbm, own_sem.at[0])
+    stage[2] = planes[late].astype(BF16)
+    spare = pltpu.make_async_copy(stage.at[2], plane_hbm, own_sem.at[0])
     spare.start()
 
     def send5(dr, d):
@@ -374,6 +375,8 @@
     stores = []
     for n, dr in enumerate(rows_order[:3]):
         group = wrap(row + dr, 4)
+        if n == 2:
+            spare.wait()
         wait(f_in.at[pl.ds(0, 7), pl.ds(0, 4)], r5.at[dr])
 
         def final(pair, carry, n=n, group=group):
@@ -393,7 +396,6 @@
         store.start()
         stores.append(store)
     wait(late_hbm.at[pl.ds(0, 7)], r5.at[last])
-    spare.wait()
     own.wait()
     for store in stores:
         store.wait()
@@ -445,7 +447,7 @@
             g = late[:, pair, :, :, quad * 128 : (quad + 1) * 128].reshape(128, 128)
             done = activate(
                 g,
-                [planes[2 * pair + o, part] for o in range(2)],
+                [planes[2 * pair + o, part].astype(F32) for o in range(2)],
                 [bias[8 * group + 2 * pair + o] for o in range(2)],
                 zit,
             )
@@ -472,7 +474,7 @@
         out_shape=(
             jax.ShapeDtypeStruct((32, 16, 32, 256), BF16),
             jax.ShapeDtypeStruct((8, 4, 2, 8, 512), BF16),
-            jax.ShapeDtypeStruct((8, 16, 32, 256), F32),
+            jax.ShapeDtypeStruct((8, 16, 32, 256), BF16),
         ),
         in_specs=[anywhere] * (len(operands) + 1),
         out_specs=(anywhere,) * 3,
@@ -514,7 +516,7 @@
         out_specs=anywhere,
         scratch_shapes=[
             pltpu.VMEM((8, 4, 2, 8, 512), BF16),
-            pltpu.VMEM((8, 16, 32, 256), F32),
+            pltpu.VMEM((8, 16, 32, 256), BF16),
             pltpu.VMEM((256, 512), BF16),
             pltpu.VMEM((8, 16, 32, 256), BF16),
             pltpu.VMEM((3, 2, 4, 16, 32, 256), BF16),

time: 85.2 us -> 84.9 us (level)
  no operation moved by 1% of the time
where the time goes in v5:
time: 84.9 us; the launch traced here: 84.8 us
  Pallas kernels  84.8 us (100%)
    pallas_call x1, Pallas kernels, body(): pl.pallas_call(transform, out_shape=(jax.ShapeDtypeStruct((32, 16, 32, 25...  76.7 us
    pallas_call x1, Pallas kernels, body(): pl.pallas_call(finish, out_shape=jax.ShapeDtypeStruct((32, 16, 32, 256),...  8.09 us

profile of v5, /device:TPU:1, one launch (start us, length us, event | category | flops | bytes accessed | tf_op | source)
XLA Modules:
  0.0 84.8 jit_solution(17540230171262643492)
XLA Ops:
  0.0 76.7 %transform.1 = (bf16[32,16,32,256]{3,2,1,0:T(8,128)(2,1)}, bf16[8,4,2,8,512]{4,3,2,1,0:T(8,128)(2,1)}, bf16[8,16,32,256]{3,2,1,0:T(8,128)(2,1)}) custom-call(bf16[32,16,32,256]{3,2,1,0:T(8,128)(2,1)} %bitcast.2, bf16[2,32,2,4,64,64]{5,4,3,2,1,0:T(8,128)(2,1)} %weight_hbm.1, bf16[128,256]{1,0:T(8,128)(2,1)} %constant.12.clone.zt_hbm, ...), custom_call_target="tpu_custom_call" | custom-call | tf_op jit(solution)/shard_map/transform/pallas_call | solution.py:472
  76.7 8.1 %finish.1 = bf16[32,16,32,256]{3,2,1,0:T(8,128)(2,1)} custom-call(bf16[32,16,32,256]{3,2,1,0:T(8,128)(2,1)} %get-tuple-element.8.early_hbm, bf16[8,4,2,8,512]{4,3,2,1,0:T(8,128)(2,1)} %get-tuple-element.9.late_hbm, bf16[8,16,32,256]{3,2,1,0:T(8,128)(2,1)} %get-tuple-element.10.plane_hbm, f32[32]{0:T(128)} %bias.1, bf16[256,512]{1,0:T(8,128)(2,1)} %constant.17.clone.zit_hbm), custom_call_target="tpu_custom_call" | custom-call | tf_op jit(solution)/shard_map/finish/pallas_call | solution.py:512
